TPU v7x, 32 devices: a whole 2x2x4 slice. The times are simulated.
32 devices in a mesh: ctx: 16 (over z, y, x), head: 2 (over core).
Axes of the slice: x: 2, y: 2, z: 4, core: 2. Of those that a mesh axis runs over, the one named last changes fastest.
Arguments:
- queries: bfloat16 [4096, 4096], P('ctx', 'head'), may hold values from -200 to 200
- span_keys: bfloat16 [4096, 4096], P('ctx', 'head'), may hold values from -6 to 6
- span_values: bfloat16 [4096, 4096], P('ctx', 'head'), may hold values from -96 to 96
- cache_keys: bfloat16 [16384, 4096], P('ctx', 'head'), may hold values from -6 to 6
- cache_values: bfloat16 [16384, 4096], P('ctx', 'head'), may hold values from -96 to 96
- land_keys: bfloat16 [256, 4096], P('ctx', 'head'), may hold values from -4.5 to 4.5
- land_values: bfloat16 [256, 4096], P('ctx', 'head'), may hold values from -96 to 96
- out_weight: bfloat16 [4096, 4096], P('head', 'ctx'), may hold values from -0.09375 to 0.09375
- selection: int32 [64, 32, 4], P('ctx', 'head'), may hold values from 0 to 255, as said below
Outputs:
- projected: bfloat16 [4096, 4096], P('ctx', 'head')
Inputs may be any that keep to these rules, and one draw needn't show every extreme that they name: `selection`: the 4 blocks of one query group and head are distinct. Count block b as owned by ctx index b // 16. Over all groups and heads of one device (one index of ctx and one of head), the selections within one owner's blocks number at most 32 and form at most 8 distinct pairs of block and head; some owner receives exactly that many of both from every device.
All inputs are finite; a program needn't handle non-finite values.
Results may differ from a plain program's by a relative error of at most 0.015.
Values may be sent and summed in bfloat16 or wider, within the bound.
No kernel may reach another device: no remote copies, remote signals or barrier semaphores. Data moves between devices by JAX's collectives and lax.ppermute only.
A program may use at most 128 MiB of HBM per device.

v0:
```python
import math
import jax
import jax.numpy as jnp
from jax import lax
from jax.sharding import PartitionSpec as P

BLOCK = 64


def local(
    queries,
    span_keys,
    span_values,
    cache_keys,
    cache_values,
    land_keys,
    land_values,
    out_weight,
    selection,
):
    query_rows, row_width = queries.shape
    groups, head_dev, pick_count = selection.shape
    head_size = row_width // head_dev
    blocks_dev = cache_keys.shape[0] // BLOCK
    devices = lax.axis_size("ctx")
    scaling = 1.0 / math.sqrt(head_size)
    query_heads = queries.reshape(query_rows, head_dev, head_size)
    run_max = jnp.full((head_dev, query_rows), -jnp.inf, jnp.float32)
    run_sum = jnp.zeros((head_dev, query_rows), jnp.float32)
    run_acc = jnp.zeros((head_dev, query_rows, head_size), jnp.float32)
    key_piece = lax.all_gather(land_keys, "ctx", axis=0, tiled=True).reshape(
        -1, head_dev, head_size
    )
    value_piece = lax.all_gather(land_values, "ctx", axis=0, tiled=True).reshape(
        -1, head_dev, head_size
    )
    scores = (
        jnp.einsum("qhd,nhd->hqn", query_heads, key_piece, preferred_element_type=jnp.float32)
        * scaling
    )
    new_max = jnp.max(scores, axis=2)
    weights = jnp.exp(scores - new_max[:, :, None])
    factor = jnp.exp(run_max - new_max)
    new_sum = run_sum * factor + jnp.sum(weights, axis=2)
    new_acc = run_acc * factor[:, :, None] + jnp.einsum(
        "hqn,nhd->hqd",
        weights.astype(jnp.bfloat16),
        value_piece,
        preferred_element_type=jnp.float32,
    )
    request_count = groups * head_dev * pick_count
    owners_flat = (selection // blocks_dev).reshape(request_count)
    block_flat = (selection % blocks_dev).reshape(request_count)
    head_flat = jnp.broadcast_to(
        jnp.arange(head_dev, dtype=jnp.int32)[None, :, None], selection.shape
    ).reshape(request_count)
    request_order = jnp.arange(request_count)
    earlier = request_order[None, :] < request_order[:, None]
    same_owner = owners_flat[:, None] == owners_flat[None, :]
    distinct_most = (head_dev * 2 * pick_count + devices - 1) // devices
    key_blocks = cache_keys.reshape(blocks_dev, BLOCK, head_dev, head_size)
    value_blocks = cache_values.reshape(blocks_dev, BLOCK, head_dev, head_size)
    asked_pairs = jnp.stack([block_flat, head_flat], axis=1)
    pair_ids = selection.reshape(request_count) * head_dev + head_flat
    same_pair = pair_ids[:, None] == pair_ids[None, :]
    is_first = jnp.logical_not(jnp.any(same_pair & earlier, axis=1))
    first_rank = jnp.sum(same_owner & earlier & is_first[None, :], axis=1)
    slot_ids = jnp.sum(jnp.where(same_pair & is_first[None, :], first_rank[None, :], 0), axis=1)
    wanted = (
        jnp.zeros((devices, distinct_most, 2), jnp.int32).at[owners_flat, slot_ids].set(asked_pairs)
    )
    asked_for = lax.all_to_all(wanted, "ctx", split_axis=0, concat_axis=0, tiled=True)
    sent_keys = key_blocks[asked_for[:, :, 0], :, asked_for[:, :, 1], :]
    sent_values = value_blocks[asked_for[:, :, 0], :, asked_for[:, :, 1], :]
    fetched_keys = lax.all_to_all(sent_keys, "ctx", split_axis=0, concat_axis=0, tiled=True)
    fetched_values = lax.all_to_all(sent_values, "ctx", split_axis=0, concat_axis=0, tiled=True)
    owner_grid = owners_flat.reshape(selection.shape)
    slot_grid = slot_ids.reshape(selection.shape)
    chosen_keys = fetched_keys[owner_grid, slot_grid]
    chosen_values = fetched_values[owner_grid, slot_grid].reshape(
        groups, head_dev, pick_count * BLOCK, head_size
    )
    query_groups = query_heads.reshape(groups, BLOCK, head_dev, head_size)
    chosen_scores = (
        jnp.einsum(
            "gqhd,ghpkd->ghqpk", query_groups, chosen_keys, preferred_element_type=jnp.float32
        )
        * scaling
    )
    chosen_scores = chosen_scores.reshape(groups, head_dev, BLOCK, pick_count * BLOCK)
    local_keys = span_keys.reshape(groups, BLOCK, head_dev, head_size)
    local_values = span_values.reshape(groups, BLOCK, head_dev, head_size)
    causal = jnp.arange(BLOCK)[:, None] >= jnp.arange(BLOCK)[None, :]
    local_scores = (
        jnp.einsum("gqhd,gkhd->ghqk", query_groups, local_keys, preferred_element_type=jnp.float32)
        * scaling
    )
    local_scores = jnp.where(causal[None, None], local_scores, -jnp.inf)
    land_top = jnp.transpose(new_max.reshape(head_dev, groups, BLOCK), (1, 0, 2))
    land_total = jnp.transpose(new_sum.reshape(head_dev, groups, BLOCK), (1, 0, 2))
    land_part = jnp.transpose(new_acc.reshape(head_dev, groups, BLOCK, head_size), (1, 0, 2, 3))
    overall_top = jnp.maximum(
        jnp.maximum(land_top, jnp.max(chosen_scores, axis=3)), jnp.max(local_scores, axis=3)
    )
    land_weight = jnp.exp(land_top - overall_top)
    chosen_weights = jnp.exp(chosen_scores - overall_top[..., None])
    local_weights = jnp.exp(local_scores - overall_top[..., None])
    denominator = (
        land_total * land_weight + jnp.sum(chosen_weights, axis=3) + jnp.sum(local_weights, axis=3)
    )
    numerator = land_part * land_weight[..., None]
    numerator = numerator + jnp.einsum(
        "ghqn,ghnd->ghqd",
        chosen_weights.astype(jnp.bfloat16),
        chosen_values,
        preferred_element_type=jnp.float32,
    )
    numerator = numerator + jnp.einsum(
        "ghqk,gkhd->ghqd",
        local_weights.astype(jnp.bfloat16),
        local_values,
        preferred_element_type=jnp.float32,
    )
    attended = (numerator / denominator[..., None]).astype(jnp.bfloat16)
    attended = jnp.transpose(attended, (0, 2, 1, 3)).reshape(query_rows, row_width)
    partial_out = jnp.dot(
        attended,
        lax.all_gather(out_weight, "ctx", axis=1, tiled=True),
        preferred_element_type=jnp.float32,
    )
    summed = lax.psum_scatter(
        partial_out.astype(jnp.bfloat16), "head", scatter_dimension=1, tiled=True
    )
    return summed


def solution(mesh):
    placed = (
        P("ctx", "head"),
        P("ctx", "head"),
        P("ctx", "head"),
        P("ctx", "head"),
        P("ctx", "head"),
        P("ctx", "head"),
        P("ctx", "head"),
        P("head", "ctx"),
        P("ctx", "head", None),
    )
    return jax.shard_map(
        local, mesh=mesh, in_specs=placed, out_specs=P("ctx", "head"), check_vma=False
    )
```

profile of v0, /device:TPU:0, one launch (start us, length us, event | category | flops | bytes accessed | tf_op | source)
XLA Modules:
  0.0 416.4 jit_solution(2511548139788343026)
XLA Ops:
  6.5 0.7 all-gather.4.cloned.1.call-update
  7.3 0.0 all-gather.6.cloned.1.call-start
  7.3 0.7 all-gather.6.cloned.1.call-update
  8.0 0.0 all-gather.8.cloned.1.call-start
  8.1 0.7 all-gather.8.cloned.1.call-update
  8.7 0.8 copy.133
  9.6 0.1 eq.33
  9.7 0.1 reshape.173
  9.8 0.1 add.97
  9.9 0.2 fusion.34
  10.1 0.1 stack_reshape.4
  10.2 0.1 reshape.174
  10.3 0.1 copy.138
  10.5 0.2 convert_reduce_fusion
  10.7 0.2 select_reduce_fusion
  10.9 11.6 %scatter_fusion = s32[16,8,2]{2,1,0:T(8,128)S(1)} fusion(s32[16,8,2]{2,1,0:T(8,128)S(1)} %broadcast_in_dim.38, s32[256]{0:T(256)S(1)} %bitcast.109, s32[256,2]{1,0:T(8,128)S(1)} %copy.138), kind=kCustom, calls=%fused_computation.4 | custom fusion | bytes 8192 | tf_op jit(solution)/shard_map/scatter | solution.py:70
  22.5 0.8 copy.139
  23.3 8.4 %all-to-all-start = ((s32[16,8,2]{1,2,0:T(2,128)}), s32[16,8,2]{1,2,0:T(2,128)S(1)}, u32[]{:S(2)}, u32[]{:S(2)}) async-start(s32[16,8,2]{1,2,0:T(2,128)} %copy.139), calls=%async_computation | async-start | bytes 32768 | tf_op jit(solution)/shard_map/all_to_all | solution.py:72
  31.7 3.6 copy.160
  35.3 3.0 copy.140
  38.3 0.7 all-to-all-done
  39.0 0.1 fusion.52
  39.1 0.1 reshape.182
  39.2 4.5 %gather_fusion = bf16[128,64,128]{2,1,0:T(8,128)(2,1)} fusion(bf16[16,64,16,128]{3,1,2,0:T(8,128)(2,1)} %copy.140, s32[128]{0:T(128)S(1)} %reshape.182), kind=kCustom, calls=%fused_computation | custom fusion | bytes 4195328 | tf_op jit(solution)/shard_map/gather | solution.py:73
  43.6 6.2 %all-to-all-start.1 = ((bf16[16,8,64,128]{3,2,1,0:T(8,128)(2,1)}), bf16[16,8,64,128]{3,2,1,0:T(8,128)(2,1)S(1)}, u32[]{:S(2)}, u32[]{:S(2)}) async-start(bf16[16,8,64,128]{3,2,1,0:T(8,128)(2,1)} %bitcast.114), calls=%async_computation.1 | async-start | bytes 4194304 | tf_op jit(solution)/shard_map/all_to_all | solution.py:75
  49.9 3.6 copy.163
  53.4 3.0 copy.146
  56.5 4.6 %gather_fusion.2 = bf16[128,64,128]{2,1,0:T(8,128)(2,1)} fusion(bf16[16,64,16,128]{3,1,2,0:T(8,128)(2,1)} %copy.146, s32[128]{0:T(128)S(1)} %reshape.182), kind=kCustom, calls=%fused_computation.2 | custom fusion | bytes 4195328 | tf_op jit(solution)/shard_map/gather | solution.py:74
  61.1 37.8 %all-to-all-done.1 = bf16[16,8,64,128]{3,2,1,0:T(8,128)(2,1)S(1)} async-done(((bf16[16,8,64,128]{3,2,1,0:T(8,128)(2,1)}), bf16[16,8,64,128]{3,2,1,0:T(8,128)(2,1)S(1)}, u32[]{:S(2)}, u32[]{:S(2)}) %all-to-all-start.1) | async-done | bytes 2097184 | tf_op jit(solution)/shard_map/all_to_all | solution.py:75
  98.9 10.5 %all-to-all-start.2 = ((bf16[16,8,64,128]{3,2,1,0:T(8,128)(2,1)}), bf16[16,8,64,128]{3,2,1,0:T(8,128)(2,1)}, u32[]{:S(2)}, u32[]{:S(2)}) async-start(bf16[16,8,64,128]{3,2,1,0:T(8,128)(2,1)} %bitcast.113), calls=%async_computation.2 | async-start | bytes 4194304 | tf_op jit(solution)/shard_map/all_to_all | solution.py:76
  109.4 0.0 reduce-scatter.2.cloned.1.call-start
  109.5 0.1 reshape.175
  109.6 0.1 reshape.188
  109.7 0.0 copy-start.5
  109.8 0.2 copy.161
  110.0 1.5 copy.162
  111.5 1.2 copy.164
  112.8 0.2 bitcast_bitcast_fusion
  113.0 2.1 fusion.12
  115.1 2.3 copy.125
  117.3 4.2 %multiply_reduce_fusion = (f32[16,256]{1,0:T(8,128)S(1)}, f32[16,256,256]{1,2,0:T(8,128)}) fusion(bf16[256,16,128]{0,2,1:T(8,128)(2,1)} %bitcast.121, bf16[256,2048]{1,0:T(8,128)(2,1)} %param.9), kind=kOutput, calls=%fused_computation.13 | convolution fusion | flops 270528512 | bytes 6307840 | tf_op jit(solution)/shard_map/qhd,nhd->hqn/dot_general | solution.py:38
  121.6 0.1 reshape.171
  121.7 2.9 fusion.2
  124.6 0.1 reduce_sum.57
  124.6 27.3 %all-gather.6.cloned.1.call-done = bf16[256,2048]{1,0:T(8,128)(2,1)} async-done(((bf16[16,2048]{1,0:T(8,128)(2,1)}), bf16[256,2048]{1,0:T(8,128)(2,1)}) %all-gather.6.cloned.1.call-update) | async-done | bytes 1048592 | tf_op jit(solution)/shard_map/all_gather | solution.py:34
  152.0 2.3 copy.128
  154.2 5.2 %fusion.13 = f32[16,256,128]{2,1,0:T(8,128)} fusion(bf16[256,16,128]{0,2,1:T(8,128)(2,1)} %bitcast.115, f32[16,256,256]{1,2,0:T(8,128)} %get-tuple-element.15, f32[16,256]{1,0:T(8,128)S(1)} %get-tuple-element.14, f32[16,256]{1,0:T(8,128)S(1)} %exponential_multiply_fusion), kind=kOutput, calls=%fused_computation.29 | convolution fusion | flops 272105472 | bytes 7372800 | tf_op jit(solution)/shard_map/hqn,nhd->hqd/dot_general | solution.py:45
  159.4 3.4 gather_fusion.1
  162.8 7.2 %bitcast_reduce_fusion = (f32[4,16,64]{2,1,0:T(8,128)S(1)}, f32[4,16,4,64,64]{4,3,2,1,0:T(8,128)}) fusion(bf16[4,16,4,64,128]{4,3,2,1,0:T(8,128)(2,1)} %bitcast.108, bf16[4,64,16,128,1]{3,2,1,0,4:T(8,128)(2,1)S(1)} %bitcast_bitcast_fusion), kind=kOutput, calls=%fused_computation.6 | convolution fusion | flops 270528512 | bytes 9453568 | tf_op jit(solution)/shard_map/gqhd,ghpkd->ghqpk/dot_general | solution.py:85
  170.0 6.8 %copy.145 = f32[4,16,64,256]{3,2,1,0:T(8,128)} copy(f32[4,16,64,256]{2,3,1,0:T(8,128)} %bitcast.107) | data formatting | bytes 8388608 | tf_op jit(solution)/shard_map/reshape | solution.py:90
  176.8 0.0 all-to-all-done.2
  176.8 5.1 %gather_fusion.3 = bf16[256,64,128]{2,1,0:T(8,128)(2,1)} fusion(bf16[16,8,64,128]{3,2,1,0:T(8,128)(2,1)} %all-to-all-done.2, s32[256]{0:T(256)S(1)} %reshape.188), kind=kCustom, calls=%fused_computation.3 | custom fusion | bytes 8390656 | tf_op jit(solution)/shard_map/gather | solution.py:80
  181.9 0.7 fusion.16
  182.6 5.5 %fusion.1 = f32[4,16,64]{2,1,0:T(8,128)S(1)} fusion(f32[4,16,4,64,64]{4,3,2,1,0:T(8,128)} %get-tuple-element.13, f32[4,16,64]{2,1,0:T(8,128)S(1)} %fusion.42), kind=kLoop, calls=%fused_computation.8 | loop fusion | flops 2093056 | bytes 4227072 | tf_op jit(solution)/shard_map/reduce_sum | solution.py:109
  188.1 0.4 copy-done.1
  188.5 1.2 fusion.6
  189.7 0.4 copy-done.3
  190.1 0.3 copy-done.6
  190.4 2.0 fusion.8
  192.4 0.7 copy.151
  193.1 197.3 %all-gather.8.cloned.1.call-done = bf16[2048,4096]{1,0:T(8,128)(2,1)} async-done(((bf16[2048,256]{1,0:T(8,128)(2,1)}), bf16[2048,4096]{1,0:T(8,128)(2,1)}) %all-gather.8.cloned.1.call-update) | async-done | bytes 16777232 | tf_op jit(solution)/shard_map/all_gather | solution.py:128
  390.4 11.5 %convolution_convert_fusion = bf16[256,4096]{1,0:T(8,128)(2,1)} fusion(bf16[2048,4096]{1,0:T(8,128)(2,1)} %all-gather.8.cloned.1.call-done, bf16[32,8,16,128]{3,2,1,0:T(8,128)(2,1)S(1)} %bitcast.127), kind=kOutput, calls=%fused_computation.9 | convolution fusion | flops 4296015872 | bytes 19922944 | tf_op jit(solution)/shard_map/dot_general | solution.py:126
  401.9 0.0 reduce-scatter.2.cloned.1.call-update
  401.9 8.0 %reduce-scatter.2.cloned.1.call-done = bf16[256,2048]{1,0:T(8,128)(2,1)} async-done(((bf16[256,4096]{1,0:T(8,128)(2,1)}), bf16[256,2048]{1,0:T(8,128)(2,1)}) %reduce-scatter.2.cloned.1.call-update) | async-done | bytes 1048592 | tf_op jit(solution)/shard_map/reduce_scatter | solution.py:131
  (23 shorter events, 0.2 us)
Async XLA Ops:
  6.5 108.5 %all-gather.4.cloned.1.call-start = ((), (), s32[]{:S(2)}) async-start(), calls=%async_computation.4 | async-start | bytes 1114112 | tf_op jit(solution)/shard_map/all_gather | solution.py:31
  7.3 144.7 %all-gather.6.cloned.1.call-start = ((), (), s32[]{:S(2)}) async-start(), calls=%async_computation.5 | async-start | bytes 1114112 | tf_op jit(solution)/shard_map/all_gather | solution.py:34
  8.0 382.4 %all-gather.8.cloned.1.call-start = ((), (), s32[]{:S(2)}) async-start(), calls=%async_computation.6 | async-start | bytes 17825792 | tf_op jit(solution)/shard_map/all_gather | solution.py:128
  23.3 15.7 %all-to-all-start = ((s32[16,8,2]{1,2,0:T(2,128)}), s32[16,8,2]{1,2,0:T(2,128)S(1)}, u32[]{:S(2)}, u32[]{:S(2)}) async-start(s32[16,8,2]{1,2,0:T(2,128)} %copy.139), calls=%async_computation | async-start | bytes 32768 | tf_op jit(solution)/shard_map/all_to_all | solution.py:72
  43.6 55.3 %all-to-all-start.1 = ((bf16[16,8,64,128]{3,2,1,0:T(8,128)(2,1)}), bf16[16,8,64,128]{3,2,1,0:T(8,128)(2,1)S(1)}, u32[]{:S(2)}, u32[]{:S(2)}) async-start(bf16[16,8,64,128]{3,2,1,0:T(8,128)(2,1)} %bitcast.114), calls=%async_computation.1 | async-start | bytes 4194304 | tf_op jit(solution)/shard_map/all_to_all | solution.py:75
  56.5 53.3 %copy-start.2 = (bf16[256,2048]{1,0:T(8,128)(2,1)S(1)}, bf16[256,2048]{1,0:T(8,128)(2,1)}, u32[]{:S(2)}) copy-start(bf16[256,2048]{1,0:T(8,128)(2,1)} %param.9) | copy-start | bytes 3145732
  98.9 77.9 %all-to-all-start.2 = ((bf16[16,8,64,128]{3,2,1,0:T(8,128)(2,1)}), bf16[16,8,64,128]{3,2,1,0:T(8,128)(2,1)}, u32[]{:S(2)}, u32[]{:S(2)}) async-start(bf16[16,8,64,128]{3,2,1,0:T(8,128)(2,1)} %bitcast.113), calls=%async_computation.2 | async-start | bytes 4194304 | tf_op jit(solution)/shard_map/all_to_all | solution.py:76
  109.4 300.5 %reduce-scatter.2.cloned.1.call-start = ((), (), s32[]{:S(2)}) async-start(), calls=%async_computation.7 | async-start | bytes 3145728 | tf_op jit(solution)/shard_map/reduce_scatter | solution.py:131
  109.7 1.8 copy-start.5
  176.8 5.1 %copy-start.4 = (f32[4,16,64,64]{2,3,1,0:T(8,128)S(1)}, f32[4,16,64,64]{2,3,1,0:T(8,128)}, u32[]{:S(2)}) copy-start(f32[4,16,64,64]{2,3,1,0:T(8,128)} %get-tuple-element.11) | copy-start | bytes 3145732
  182.6 5.5 %copy-start = (f32[4,16,64,256]{3,2,1,0:T(8,128)S(1)}, f32[4,16,64,256]{3,2,1,0:T(8,128)}, u32[]{:S(2)}) copy-start(f32[4,16,64,256]{3,2,1,0:T(8,128)} %copy.145) | copy-start | bytes 12582916
  182.6 5.9 %copy-start.1 = (bf16[256,64,128]{2,1,0:T(8,128)(2,1)S(1)}, bf16[256,64,128]{2,1,0:T(8,128)(2,1)}, u32[]{:S(2)}) copy-start(bf16[256,64,128]{2,1,0:T(8,128)(2,1)} %gather_fusion.3) | copy-start | bytes 12582916
  188.5 1.6 copy-start.3
  188.5 1.9 copy-start.6
Sparse Core Ops, SparseCore 0:
  10.1 65.8 all-gather.3
  78.8 73.1 all-gather.5
  154.7 235.6 all-gather.7
  402.1 7.7 reduce-scatter.1
where the time goes:
time: 417 us; the launch traced here: 416 us
  waiting for transfers between devices  273 us (65%)
  local copies, waits for them, and re-layouts  61.3 us (15%)
  matrix products  33.5 us (8%)
  starting transfers between devices  25.2 us (6%)
  between operations  13.4 us (3%)
  other arithmetic  9.83 us (2%)
    all_gather x1, waiting for transfers between devices, local(): lax.all_gather(out_weight, 'ctx', axis=1, tiled=True)  197 us
    all_to_all x1, waiting for transfers between devices, local(): lax.all_to_all(sent_keys, 'ctx', split_axis=0, concat_axis=0, tiled=True)  37.8 us
    all_gather x1, waiting for transfers between devices, local(): lax.all_gather(land_values, 'ctx', axis=0, tiled=True)  27.3 us
    scatter x2, local copies, waits for them, and re-layouts, local(): jnp.zeros((devices, distinct_most, 2), jnp.int32).at[owners_flat, slot_ids]  12.4 us
    unnamed x20, local copies, waits for them, and re-layouts  12 us
    dot_general x1, matrix products, local(): jnp.dot(attended, lax.all_gather(out_weight, 'ctx', axis=1, tiled=True),...  11.5 us
    all_to_all x1, starting transfers between devices, local(): lax.all_to_all(sent_values, 'ctx', split_axis=0, concat_axis=0, tiled=True)  10.5 us
    all_to_all x1, starting transfers between devices, local(): lax.all_to_all(wanted, 'ctx', split_axis=0, concat_axis=0, tiled=True)  8.35 us
  transfers between devices with their start and end apart: 7, of which 5 were waited for; matrix products, arithmetic and copies ran while one was open for 22% of the time, Pallas kernels for 0%

commit v1 on v0

--- a/solution.py
+++ b/solution.py
@@ -125,7 +125,7 @@
     attended = jnp.transpose(attended, (0, 2, 1, 3)).reshape(query_rows, row_width)
     partial_out = jnp.dot(
         attended,
-        lax.all_gather(out_weight, "ctx", axis=1, tiled=True),
+        jnp.concatenate(lax.all_gather(out_weight, "ctx"), axis=1),
         preferred_element_type=jnp.float32,
     )
     summed = lax.psum_scatter(

time: 417 us -> 402 us (0.964)
  waiting for transfers between devices: 273 us -> 230 us
  local copies, waits for them, and re-layouts: 61.3 us -> 83 us
  matrix products: 33.5 us -> 40.1 us
    all_gather x1, waiting for transfers between devices: 197 us -> 154 us  [local(): lax.all_gather(out_weight, 'ctx')]
    reshape x0 -> x1, local copies, waits for them, and re-layouts: none -> 21.7 us  [local(): jnp.concatenate(lax.all_gather(out_weight, 'ctx'), axis=1)]
    dot_general x1, matrix products: 11.5 us -> 18 us  [local(): jnp.dot(attended, jnp.concatenate(lax.all_gather(out_weight, 'ctx'), axis...]
  transfers between devices with their start and end apart: 7 -> 7, of which waited for: 5 -> 5; matrix products, arithmetic and copies ran while one was open for 22% -> 23% of each run, Pallas kernels for 0% -> 0%
where the time goes in v1:
time: 402 us; the launch traced here: 401 us
  waiting for transfers between devices  230 us (57%)
  local copies, waits for them, and re-layouts  83 us (21%)
  matrix products  40.1 us (10%)
  starting transfers between devices  25.2 us (6%)
  between operations  13.4 us (3%)
  other arithmetic  9.87 us (2%)
    all_gather x1, waiting for transfers between devices, local(): lax.all_gather(out_weight, 'ctx')  154 us
    all_to_all x1, waiting for transfers between devices, local(): lax.all_to_all(sent_keys, 'ctx', split_axis=0, concat_axis=0, tiled=True)  37.8 us
    all_gather x1, waiting for transfers between devices, local(): lax.all_gather(land_values, 'ctx', axis=0, tiled=True)  27.3 us
    reshape x1, local copies, waits for them, and re-layouts, local(): jnp.concatenate(lax.all_gather(out_weight, 'ctx'), axis=1)  21.7 us
    dot_general x1, matrix products, local(): jnp.dot(attended, jnp.concatenate(lax.all_gather(out_weight, 'ctx'), axis...  18 us
    scatter x2, local copies, waits for them, and re-layouts, local(): jnp.zeros((devices, distinct_most, 2), jnp.int32).at[owners_flat, slot_ids]  12.4 us
    unnamed x20, local copies, waits for them, and re-layouts  11.9 us
    all_to_all x1, starting transfers between devices, local(): lax.all_to_all(sent_values, 'ctx', split_axis=0, concat_axis=0, tiled=True)  10.5 us
  transfers between devices with their start and end apart: 7, of which 5 were waited for; matrix products, arithmetic and copies ran while one was open for 23% of the time, Pallas kernels for 0%

profile of v1, /device:TPU:0, one launch (start us, length us, event | category | flops | bytes accessed | tf_op | source)
XLA Modules:
  0.0 401.2 jit_solution(17739332547592085745)
XLA Ops:
  6.5 0.7 all-gather.5.cloned.1.call-update
  7.3 0.0 all-gather.7.cloned.1.call-start
  7.3 0.7 all-gather.7.cloned.1.call-update
  8.0 0.0 all-gather.9.cloned.1.call-start
  8.1 0.7 all-gather.9.cloned.1.call-update
  8.7 0.8 copy.136
  9.6 0.1 eq.33
  9.7 0.1 reshape.179
  9.8 0.1 add.97
  9.9 0.2 fusion.34
  10.1 0.1 stack_reshape.4
  10.2 0.1 reshape.180
  10.3 0.1 copy.141
  10.5 0.2 convert_reduce_fusion
  10.7 0.2 select_reduce_fusion
  10.9 11.6 %scatter_fusion = s32[16,8,2]{2,1,0:T(8,128)S(1)} fusion(s32[16,8,2]{2,1,0:T(8,128)S(1)} %broadcast_in_dim.38, s32[256]{0:T(256)S(1)} %bitcast.113, s32[256,2]{1,0:T(8,128)S(1)} %copy.141), kind=kCustom, calls=%fused_computation.4 | custom fusion | bytes 8192 | tf_op jit(solution)/shard_map/scatter | solution.py:70
  22.5 0.8 copy.142
  23.3 8.4 %all-to-all-start = ((s32[16,8,2]{1,2,0:T(2,128)}), s32[16,8,2]{1,2,0:T(2,128)S(1)}, u32[]{:S(2)}, u32[]{:S(2)}) async-start(s32[16,8,2]{1,2,0:T(2,128)} %copy.142), calls=%async_computation | async-start | bytes 32768 | tf_op jit(solution)/shard_map/all_to_all | solution.py:72
  31.7 3.6 copy.164
  35.3 3.0 copy.143
  38.3 0.7 all-to-all-done
  39.0 0.1 fusion.52
  39.1 0.1 reshape.190
  39.2 4.5 %gather_fusion = bf16[128,64,128]{2,1,0:T(8,128)(2,1)} fusion(bf16[16,64,16,128]{3,1,2,0:T(8,128)(2,1)} %copy.143, s32[128]{0:T(128)S(1)} %reshape.190), kind=kCustom, calls=%fused_computation | custom fusion | bytes 4195328 | tf_op jit(solution)/shard_map/gather | solution.py:73
  43.6 6.2 %all-to-all-start.1 = ((bf16[16,8,64,128]{3,2,1,0:T(8,128)(2,1)}), bf16[16,8,64,128]{3,2,1,0:T(8,128)(2,1)S(1)}, u32[]{:S(2)}, u32[]{:S(2)}) async-start(bf16[16,8,64,128]{3,2,1,0:T(8,128)(2,1)} %bitcast.120), calls=%async_computation.1 | async-start | bytes 4194304 | tf_op jit(solution)/shard_map/all_to_all | solution.py:75
  49.9 3.6 copy.167
  53.4 3.0 copy.149
  56.5 4.6 %gather_fusion.2 = bf16[128,64,128]{2,1,0:T(8,128)(2,1)} fusion(bf16[16,64,16,128]{3,1,2,0:T(8,128)(2,1)} %copy.149, s32[128]{0:T(128)S(1)} %reshape.190), kind=kCustom, calls=%fused_computation.2 | custom fusion | bytes 4195328 | tf_op jit(solution)/shard_map/gather | solution.py:74
  61.1 37.8 %all-to-all-done.1 = bf16[16,8,64,128]{3,2,1,0:T(8,128)(2,1)S(1)} async-done(((bf16[16,8,64,128]{3,2,1,0:T(8,128)(2,1)}), bf16[16,8,64,128]{3,2,1,0:T(8,128)(2,1)S(1)}, u32[]{:S(2)}, u32[]{:S(2)}) %all-to-all-start.1) | async-done | bytes 2097184 | tf_op jit(solution)/shard_map/all_to_all | solution.py:75
  98.9 10.5 %all-to-all-start.2 = ((bf16[16,8,64,128]{3,2,1,0:T(8,128)(2,1)}), bf16[16,8,64,128]{3,2,1,0:T(8,128)(2,1)}, u32[]{:S(2)}, u32[]{:S(2)}) async-start(bf16[16,8,64,128]{3,2,1,0:T(8,128)(2,1)} %bitcast.119), calls=%async_computation.2 | async-start | bytes 4194304 | tf_op jit(solution)/shard_map/all_to_all | solution.py:76
  109.4 0.0 reduce-scatter.2.cloned.1.call-start
  109.5 0.1 reshape.181
  109.6 0.1 reshape.196
  109.7 0.0 copy-start.5
  109.8 0.2 copy.165
  110.0 1.5 copy.166
  111.5 1.2 copy.168
  112.8 0.2 bitcast_bitcast_fusion
  113.0 2.1 fusion.12
  115.1 2.3 copy.128
  117.3 4.2 %multiply_reduce_fusion = (f32[16,256]{1,0:T(8,128)S(1)}, f32[16,256,256]{1,2,0:T(8,128)}) fusion(bf16[256,16,128]{0,2,1:T(8,128)(2,1)} %bitcast.127, bf16[256,2048]{1,0:T(8,128)(2,1)} %param.9), kind=kOutput, calls=%fused_computation.13 | convolution fusion | flops 270528512 | bytes 6307840 | tf_op jit(solution)/shard_map/qhd,nhd->hqn/dot_general | solution.py:38
  121.6 0.1 reshape.177
  121.7 2.9 fusion.2
  124.6 0.1 reduce_sum.57
  124.6 27.3 %all-gather.7.cloned.1.call-done = bf16[256,2048]{1,0:T(8,128)(2,1)} async-done(((bf16[16,2048]{1,0:T(8,128)(2,1)}), bf16[256,2048]{1,0:T(8,128)(2,1)}) %all-gather.7.cloned.1.call-update) | async-done | bytes 1048592 | tf_op jit(solution)/shard_map/all_gather | solution.py:34
  152.0 2.3 copy.131
  154.2 5.2 %fusion.13 = f32[16,256,128]{2,1,0:T(8,128)} fusion(bf16[256,16,128]{0,2,1:T(8,128)(2,1)} %bitcast.121, f32[16,256,256]{1,2,0:T(8,128)} %get-tuple-element.15, f32[16,256]{1,0:T(8,128)S(1)} %get-tuple-element.14, f32[16,256]{1,0:T(8,128)S(1)} %exponential_multiply_fusion), kind=kOutput, calls=%fused_computation.29 | convolution fusion | flops 272105472 | bytes 7372800 | tf_op jit(solution)/shard_map/hqn,nhd->hqd/dot_general | solution.py:45
  159.4 3.4 gather_fusion.1
  162.8 7.2 %bitcast_reduce_fusion = (f32[4,16,64]{2,1,0:T(8,128)S(1)}, f32[4,16,4,64,64]{4,3,2,1,0:T(8,128)}) fusion(bf16[4,16,4,64,128]{4,3,2,1,0:T(8,128)(2,1)} %bitcast.112, bf16[4,64,16,128,1]{3,2,1,0,4:T(8,128)(2,1)S(1)} %bitcast_bitcast_fusion), kind=kOutput, calls=%fused_computation.6 | convolution fusion | flops 270528512 | bytes 9453568 | tf_op jit(solution)/shard_map/gqhd,ghpkd->ghqpk/dot_general | solution.py:85
  170.0 6.8 %copy.148 = f32[4,16,64,256]{3,2,1,0:T(8,128)} copy(f32[4,16,64,256]{2,3,1,0:T(8,128)} %bitcast.111) | data formatting | bytes 8388608 | tf_op jit(solution)/shard_map/reshape | solution.py:90
  176.9 5.1 %gather_fusion.3 = bf16[256,64,128]{2,1,0:T(8,128)(2,1)} fusion(bf16[16,8,64,128]{3,2,1,0:T(8,128)(2,1)} %all-to-all-done.2, s32[256]{0:T(256)S(1)} %reshape.196), kind=kCustom, calls=%fused_computation.3 | custom fusion | bytes 8390656 | tf_op jit(solution)/shard_map/gather | solution.py:80
  182.0 0.7 fusion.16
  182.7 5.5 %fusion.1 = f32[4,16,64]{2,1,0:T(8,128)S(1)} fusion(f32[4,16,4,64,64]{4,3,2,1,0:T(8,128)} %get-tuple-element.13, f32[4,16,64]{2,1,0:T(8,128)S(1)} %fusion.42), kind=kLoop, calls=%fused_computation.8 | loop fusion | flops 2093056 | bytes 4227072 | tf_op jit(solution)/shard_map/reduce_sum | solution.py:109
  188.2 0.3 copy-done.1
  188.5 1.2 fusion.6
  189.7 0.4 copy-done.3
  190.1 0.3 copy-done.6
  190.4 2.0 fusion.8
  192.4 0.7 copy.154
  193.1 153.7 %all-gather.9.cloned.1.call-done = bf16[32768,256]{1,0:T(8,128)(2,1)} async-done(((bf16[2048,256]{1,0:T(8,128)(2,1)}), bf16[32768,256]{1,0:T(8,128)(2,1)}) %all-gather.9.cloned.1.call-update) | async-done | bytes 16777232 | tf_op jit(solution)/shard_map/all_gather | solution.py:128
  346.9 21.7 %copy.155 = bf16[2048,16,256]{0,2,1:T(8,128)(2,1)} copy(bf16[2048,16,256]{2,0,1:T(8,128)(2,1)} %bitcast.114) | data formatting | bytes 33554432 | tf_op jit(solution)/shard_map/reshape | solution.py:128
  368.6 18.0 %convolution_convert_fusion = bf16[256,4096]{1,0:T(8,128)(2,1)} fusion(bf16[2048,4096]{0,1:T(8,128)(2,1)} %bitcast.115, bf16[32,8,16,128]{3,2,1,0:T(8,128)(2,1)S(1)} %bitcast.133), kind=kOutput, calls=%fused_computation.9 | convolution fusion | flops 4296015872 | bytes 19922944 | tf_op jit(solution)/shard_map/dot_general | solution.py:126
  386.6 0.0 reduce-scatter.2.cloned.1.call-update
  386.7 8.0 %reduce-scatter.2.cloned.1.call-done = bf16[256,2048]{1,0:T(8,128)(2,1)} async-done(((bf16[256,4096]{1,0:T(8,128)(2,1)}), bf16[256,2048]{1,0:T(8,128)(2,1)}) %reduce-scatter.2.cloned.1.call-update) | async-done | bytes 1048592 | tf_op jit(solution)/shard_map/reduce_scatter | solution.py:131
  (24 shorter events, 0.2 us)
Async XLA Ops:
  6.5 108.5 %all-gather.5.cloned.1.call-start = ((), (), s32[]{:S(2)}) async-start(), calls=%async_computation.4 | async-start | bytes 1114112 | tf_op jit(solution)/shard_map/all_gather | solution.py:31
  7.3 144.7 %all-gather.7.cloned.1.call-start = ((), (), s32[]{:S(2)}) async-start(), calls=%async_computation.5 | async-start | bytes 1114112 | tf_op jit(solution)/shard_map/all_gather | solution.py:34
  8.0 338.9 %all-gather.9.cloned.1.call-start = ((), (), s32[]{:S(2)}) async-start(), calls=%async_computation.7 | async-start | bytes 17825792 | tf_op jit(solution)/shard_map/all_gather | solution.py:128
  23.3 15.7 %all-to-all-start = ((s32[16,8,2]{1,2,0:T(2,128)}), s32[16,8,2]{1,2,0:T(2,128)S(1)}, u32[]{:S(2)}, u32[]{:S(2)}) async-start(s32[16,8,2]{1,2,0:T(2,128)} %copy.142), calls=%async_computation | async-start | bytes 32768 | tf_op jit(solution)/shard_map/all_to_all | solution.py:72
  43.6 55.3 %all-to-all-start.1 = ((bf16[16,8,64,128]{3,2,1,0:T(8,128)(2,1)}), bf16[16,8,64,128]{3,2,1,0:T(8,128)(2,1)S(1)}, u32[]{:S(2)}, u32[]{:S(2)}) async-start(bf16[16,8,64,128]{3,2,1,0:T(8,128)(2,1)} %bitcast.120), calls=%async_computation.1 | async-start | bytes 4194304 | tf_op jit(solution)/shard_map/all_to_all | solution.py:75
  56.5 53.3 %copy-start.2 = (bf16[256,2048]{1,0:T(8,128)(2,1)S(1)}, bf16[256,2048]{1,0:T(8,128)(2,1)}, u32[]{:S(2)}) copy-start(bf16[256,2048]{1,0:T(8,128)(2,1)} %param.9) | copy-start | bytes 3145732
  98.9 78.0 %all-to-all-start.2 = ((bf16[16,8,64,128]{3,2,1,0:T(8,128)(2,1)}), bf16[16,8,64,128]{3,2,1,0:T(8,128)(2,1)}, u32[]{:S(2)}, u32[]{:S(2)}) async-start(bf16[16,8,64,128]{3,2,1,0:T(8,128)(2,1)} %bitcast.119), calls=%async_computation.2 | async-start | bytes 4194304 | tf_op jit(solution)/shard_map/all_to_all | solution.py:76
  109.4 285.2 %reduce-scatter.2.cloned.1.call-start = ((), (), s32[]{:S(2)}) async-start(), calls=%async_computation.6 | async-start | bytes 3145728 | tf_op jit(solution)/shard_map/reduce_scatter | solution.py:131
  109.7 1.8 copy-start.5
  176.9 5.1 %copy-start.4 = (f32[4,16,64,64]{2,3,1,0:T(8,128)S(1)}, f32[4,16,64,64]{2,3,1,0:T(8,128)}, u32[]{:S(2)}) copy-start(f32[4,16,64,64]{2,3,1,0:T(8,128)} %get-tuple-element.11) | copy-start | bytes 3145732
  182.6 5.6 %copy-start = (f32[4,16,64,256]{3,2,1,0:T(8,128)S(1)}, f32[4,16,64,256]{3,2,1,0:T(8,128)}, u32[]{:S(2)}) copy-start(f32[4,16,64,256]{3,2,1,0:T(8,128)} %copy.148) | copy-start | bytes 12582916
  182.7 5.9 %copy-start.1 = (bf16[256,64,128]{2,1,0:T(8,128)(2,1)S(1)}, bf16[256,64,128]{2,1,0:T(8,128)(2,1)}, u32[]{:S(2)}) copy-start(bf16[256,64,128]{2,1,0:T(8,128)(2,1)} %gather_fusion.3) | copy-start | bytes 12582916
  188.5 1.6 copy-start.3
  188.5 1.9 copy-start.6
Sparse Core Ops, SparseCore 0:
  10.1 65.8 all-gather.4
  78.8 73.1 all-gather.6
  154.7 192.0 all-gather.8
  386.8 7.8 reduce-scatter.1
